TPU v7x, 32 devices: a whole 2x2x4 slice. The times are simulated.
32 devices in a mesh: dp: 4 (over x, core), hist: 8 (over z, y).
Axes of the slice: x: 2, y: 2, z: 4, core: 2. Of those that a mesh axis runs over, the one named last changes fastest.
Arguments:
- candidates: bfloat16 [16, 512, 128], P('dp', 'hist'), may hold values from -150 to 150
- history: bfloat16 [16, 16384, 128], P('dp', 'hist'), may hold values from -6 to 6
- projections: bfloat16 [4, 128, 128], P(None, 'dp'), may hold values from -0.5 to 0.5
- lengths: int32 [16], P('dp'), may hold values from 8193 to 16384
- selected: int32 [16, 64], P('dp'), may hold values from 0 to 127, as said below
Outputs:
- interest: bfloat16 [16, 512, 128], P('dp', 'hist')
Inputs may be any that keep to these rules, and one draw needn't show every extreme that they name: `selected`: each row names 64 different history blocks.
All inputs are finite; a program needn't handle non-finite values.
Results may differ from a plain program's by a relative error of at most 0.008.
The roundings to bfloat16 on the way count: a program that leaves them out, or rounds other values in their place, can miss the bound.
Values may be sent and summed in bfloat16 or wider, within the bound.
A program may use at most 128 MiB of HBM per device.

v0:
```python
import functools
import math

import jax
import jax.numpy as jnp
from jax import lax
from jax.experimental import pallas as pl
from jax.experimental.pallas import tpu as pltpu
from jax.sharding import PartitionSpec as P

H = 4
BLOCK = 128
PAIR = 2
TRIP = 2
PAD = 1 << 20
LAG = 2
SAMPLE = 32
SMALL = 2.0**-30
LARGE = 2.0**100
ROOM = 40 << 20
LOW = -1e30


def gather_kernel(
    n,
    ranks,
    lengths,
    cand_in,
    proj_in,
    hist,
    picks_in,
    all_proj,
    high,
    low,
    keys,
    values,
    flags,
    cand,
    proj,
    picks,
    all_cand,
    rows_in,
    own_sem,
    arg_sem,
    in_sem,
    z_send,
    z_recv,
    y_send,
    y_recv,
    w_send,
    w_recv,
):
    mesh_id = pl.DeviceIdType.MESH
    me, rank = lax.axis_index("hist"), lax.axis_index("dp")
    line = n // 2
    side, spot = lax.rem(me, 2), me // 2
    users, own = cand.shape[0], cand.shape[1]
    rows = proj.shape[1]
    own_rows, embed = hist.shape[1], hist.shape[2]
    blocks = own_rows // BLOCK
    factor = math.log2(math.e) / math.sqrt(embed // H)

    def place(u, owner):
        return all_cand.at[u, pl.ds(pl.multiple_of(owner * own, own), own), :]

    loads = [
        pltpu.make_async_copy(src, dst, arg_sem.at[k])
        for k, (src, dst) in enumerate(((proj_in, proj), (cand_in, cand), (picks_in, picks)))
    ]
    strip = all_proj.at[:, pl.ds(pl.multiple_of(rank * rows, rows), rows), :]
    locals_ = [pltpu.make_async_copy(proj_in, strip, own_sem.at[users])]
    locals_ += [pltpu.make_async_copy(cand_in.at[u], place(u, me), own_sem.at[u]) for u in range(users)]
    fetches = [pltpu.make_async_copy(hist.at[u], rows_in.at[u], in_sem.at[u]) for u in range(users)]
    for copy in loads + locals_ + fetches:
        copy.start()
    partner = spot * 2 + (1 - side)
    peers = [lax.rem(spot + k, line) * 2 + side for k in range(1, line)]
    mates = [lax.rem(rank + k, ranks) for k in range(1, ranks)]

    barrier = pltpu.get_barrier_semaphore()
    for peer in [partner] + peers:
        pl.semaphore_signal(barrier, inc=1, device_id={"hist": peer}, device_id_type=mesh_id)
    for mate in mates:
        pl.semaphore_signal(barrier, inc=1, device_id={"dp": mate}, device_id_type=mesh_id)
    pl.semaphore_wait(barrier, line + ranks - 1)

    loads[0].wait()
    loads[1].wait()
    weight_copies = []
    for k, mate in enumerate(mates):
        copy = pltpu.make_async_remote_copy(
            proj, strip, w_send.at[k], w_recv.at[k], device_id={"dp": mate}, device_id_type=mesh_id
        )
        copy.start()
        weight_copies.append(copy)
    across, along = {}, {}
    for u in range(users):
        for k, peer in enumerate(peers):
            copy = pltpu.make_async_remote_copy(
                cand.at[u],
                place(u, me),
                z_send.at[k, u],
                z_recv.at[k, u],
                device_id={"hist": peer},
                device_id_type=mesh_id,
            )
            copy.start()
            along[k, u] = copy
        copy = pltpu.make_async_remote_copy(
            cand.at[u],
            place(u, me),
            y_send.at[0, u],
            y_recv.at[0, u],
            device_id={"hist": partner},
            device_id_type=mesh_id,
        )
        copy.start()
        across[0, u] = copy
    loads[2].wait()
    spans = lax.broadcasted_iota(jnp.int32, (users, 128), 0)
    limits = jnp.zeros((users, 128), jnp.int32)
    for u in range(users):
        limits = jnp.where(spans == u, lengths[u], limits)
    lane = lax.broadcasted_iota(jnp.int32, (users, 128), 1)
    found = jnp.zeros((users, 128), jnp.int32)
    chosen = picks[...]
    for b in range(blocks):
        hit = jnp.max(jnp.where(chosen == me * blocks + b, 1.0, 0.0), axis=1, keepdims=True)
        found = jnp.where(jnp.logical_and(lane == b, hit > 0.0), 1, found)
    flags[...] = jnp.where((me * blocks + lane) * BLOCK < limits, found, 0)
    locals_[0].wait()
    for copy in weight_copies:
        copy.wait()
    key_weight, value_weight = all_proj[1], all_proj[2]
    shape = (blocks, BLOCK, embed)
    places = lax.broadcasted_iota(jnp.int32, shape, 0) * BLOCK + lax.broadcasted_iota(jnp.int32, shape, 1)
    places = places + me * own_rows
    for u in range(users):
        for k in range(line - 1):
            along[k, u].wait_recv()
            source = lax.rem(spot + line - (k + 1), line) * 2 + side
            copy = pltpu.make_async_remote_copy(
                place(u, source),
                place(u, source),
                y_send.at[k + 1, u],
                y_recv.at[k + 1, u],
                device_id={"hist": partner},
                device_id_type=mesh_id,
            )
            copy.start()
            across[k + 1, u] = copy
        fetches[u].wait()
        block_rows = rows_in[u].reshape(shape).astype(jnp.float32)
        alive = places < lengths[u]
        safe = jnp.where(alive, block_rows, block_rows[:, 0:1, :]).astype(jnp.bfloat16).reshape(own_rows, embed)
        kept = jnp.where(alive, block_rows, 0.0).astype(jnp.bfloat16).reshape(own_rows, embed)
        keys[u] = jnp.dot(safe, key_weight, preferred_element_type=jnp.float32).astype(jnp.bfloat16)
        values[u] = lax.dot_general(
            value_weight, kept, (((0,), (1,)), ((), ())), preferred_element_type=jnp.float32
        ).astype(jnp.bfloat16)
    for u in range(users):
        for k in range(line):
            across[k, u].wait_recv()
        locals_[1 + u].wait()
        plain = lax.dot_general(
            all_proj[0], all_cand[u], (((0,), (1,)), ((), ())), preferred_element_type=jnp.float32
        ).astype(jnp.bfloat16)
        scaled = plain.astype(jnp.float32) * factor
        upper = scaled.astype(jnp.bfloat16)
        high[u] = upper
        low[u] = (scaled - upper.astype(jnp.float32)).astype(jnp.bfloat16)
    for copy in list(along.values()) + list(across.values()):
        copy.wait_send()


def attend_kernel(
    own_cands,
    lengths,
    flags,
    base,
    high,
    low,
    keys,
    values,
    parts,
    stats,
    marks,
    acc,
    shift,
    top,
    probs,
    slots,
    owners,
):
    users, embed, cands = high.shape
    head = embed // H
    half = embed // 2
    tall = acc[0].shape[1]
    blocks = keys.shape[1] // BLOCK
    first = base[0]

    owners[0] = 0
    slots[0] = PAD
    slots[1] = PAD
    item = jnp.int32(1)
    begins, counts = [], []
    for u in range(users):
        last = jnp.int32(0)
        at = item * PAIR
        begins.append(item)
        for b in range(blocks):
            alive = flags[u, b]
            slots[at] = b
            at = at + alive
            last = jnp.where(alive > 0, b, last)
        for k in range(3 * PAIR):
            slots[at + k] = last + PAD
        for p in range(blocks // PAIR + 3):
            owners[item + p] = u
        counts.append(at - item * PAIR)
        item = (at + 1) // PAIR
    trips = (item - 1 + TRIP - 1) // TRIP

    def start_of(slot):
        block = jnp.where(slot >= PAD, slot - PAD, slot)
        return pl.multiple_of(block * BLOCK, BLOCK)

    column = lax.broadcasted_iota(jnp.int32, (1, embed), 1)
    group = [(h * head) // half for h in range(H)]
    spot = [(1 - group[h]) * half + (h - group[h] * (H // 2)) * 16 for h in range(H)]
    mine = [jnp.where(column // head == h, 1.0, 0.0).astype(jnp.bfloat16) for h in range(H)]
    mark = [jnp.where(column == spot[h], 1.0, 0.0).astype(jnp.bfloat16) for h in range(H)]
    lead = lax.broadcasted_iota(jnp.int32, (16, cands), 0) == 0

    for u in range(users):
        sample = keys[u, pl.ds(start_of(slots[begins[u] * PAIR]), SAMPLE), :]
        guess = jnp.dot(
            jnp.concatenate([sample * mine[h] for h in range(H)], axis=0), high[u], preferred_element_type=jnp.float32
        )
        for h in range(H):
            most = jnp.max(guess[h * SAMPLE : (h + 1) * SAMPLE, :], axis=0, keepdims=True)
            most = most.astype(jnp.bfloat16).astype(jnp.float32)
            shift[h][u] = most
            marks[h][u] = jnp.where(lead, -most, 0.0).astype(jnp.bfloat16)
    for h in range(H):
        acc[h][...] = jnp.zeros(acc[h].shape, jnp.float32)
    for k in range(2):
        probs[2 + k][...] = jnp.zeros(probs[2 + k].shape, jnp.bfloat16)

    right = lax.broadcasted_iota(jnp.int32, (tall - head, BLOCK), 1)
    under = lax.broadcasted_iota(jnp.int32, (tall - head, BLOCK), 0)
    right = jnp.where(under == 0, right, jnp.iinfo(jnp.int32).max)

    def scores(i, h):
        user = owners[i]
        key = jnp.concatenate([keys[user, pl.ds(start_of(slots[i * PAIR + k]), BLOCK), :] for k in range(PAIR)], axis=0)
        key = key * mine[h]
        pieces = [high[user]]
        if spot[h] > 0:
            pieces.append(low[user, 0 : spot[h], :])
        pieces += [marks[h][user], low[user, spot[h] + 16 : embed, :]]
        query = jnp.concatenate(pieces, axis=0)
        return jnp.dot(jnp.concatenate([key, key + mark[h]], axis=1), query, preferred_element_type=jnp.float32)

    def gain(i, h, prob):
        user = owners[i]
        pieces = []
        for k in range(PAIR):
            slot = slots[i * PAIR + k]
            start = start_of(slot)
            limit = jnp.where(slot >= PAD, 0, lengths[user] - (start + first * BLOCK))
            one = jnp.where(right < limit, 1.0, 0.0).astype(jnp.bfloat16)
            value = values[user, h * head : (h + 1) * head, pl.ds(start, BLOCK)]
            value = jnp.where(slot >= PAD, jnp.zeros_like(value), value)
            pieces.append(jnp.concatenate([value, one], axis=0))
        return jnp.dot(jnp.concatenate(pieces, axis=1), prob, preferred_element_type=jnp.float32)

    @pl.loop(0, trips)
    def _(step):
        begin = step * TRIP + 1
        for s in range(TRIP * H):
            late, head_late = begin + (s + 2 * H - LAG) // H - 2, (s + H - LAG) % H
            probs[s % 4][...] = jnp.exp2(scores(begin + s // H, s % H)).astype(jnp.bfloat16)
            acc[head_late][owners[late]] += gain(late, head_late, probs[(s - LAG) % 4][...])

    for k in range(LAG):
        h = H - LAG + k
        user = owners[trips * TRIP]
        acc[h][user] += gain(trips * TRIP, h, probs[(TRIP * H - LAG + k) % 4][...])

    wrong = jnp.zeros((1, cands), jnp.float32)
    for u in range(users):
        for h in range(H):
            amount = acc[h][u, head : head + 1, :]
            fine = jnp.logical_and(amount > SMALL, amount < LARGE)
            wrong = jnp.maximum(wrong, jnp.where(fine, 0.0, jnp.where(counts[u] > 0, 1.0, 0.0)))

    @pl.when(jnp.max(wrong) > 0.0)
    def _():
        for h in range(H):
            acc[h][...] = jnp.zeros(acc[h].shape, jnp.float32)
            top[h][...] = jnp.full(top[h].shape, LOW, jnp.float32)

        @pl.loop(1, item)
        def _(i):
            user = owners[i]
            for h in range(H):
                got = scores(i, h)
                before = top[h][user]
                peak = jnp.maximum(before, jnp.max(got, axis=0, keepdims=True))
                prob = jnp.exp2(got - peak).astype(jnp.bfloat16)
                acc[h][user] = acc[h][user] * jnp.exp2(before - peak) + gain(i, h, prob)
                top[h][user] = peak

        for h in range(H):
            shift[h][...] = shift[h][...] + top[h][...]

    means, logs = [], []
    for u in range(users):
        rows, row_logs = [], []
        for h in range(H):
            amount = acc[h][u, head : head + 1, :]
            some = jnp.logical_and(counts[u] > 0, amount > 0.0)
            safe = jnp.where(some, amount, 1.0)
            mean = jnp.where(some, acc[h][u, 0:head, :] * (1.0 / safe), 0.0)
            rows.append(mean.astype(jnp.bfloat16))
            row_logs.append(jnp.where(some, shift[h][u] + jnp.log2(safe), LOW))
        means.append(jnp.concatenate(rows, axis=0))
        logs.append(jnp.concatenate(row_logs, axis=0))
    for dest in range(parts.shape[0]):
        at = slice(dest * own_cands, (dest + 1) * own_cands)
        to = slice(0, users * own_cands)
        parts[dest, :, to] = jnp.concatenate([m[:, at] for m in means], axis=1)
        stats[dest, :, to] = jnp.concatenate([m[:, at] for m in logs], axis=1)


def combine_kernel(n, parts, stats, out_weight, result, got, got_stats, send_a, recv_a, send_b, recv_b):
    me = lax.axis_index("hist")
    barrier = pltpu.get_barrier_semaphore()
    for k in range(1, n):
        pl.semaphore_signal(
            barrier, inc=1, device_id={"hist": lax.rem(me + k, n)}, device_id_type=pl.DeviceIdType.MESH
        )
    pl.semaphore_wait(barrier, n - 1)
    copies = []
    for k in range(1, n):
        peer = lax.rem(me + k, n)
        for src, dst, send, recv in ((stats, got_stats, send_b, recv_b), (parts, got, send_a, recv_a)):
            copy = pltpu.make_async_remote_copy(
                src_ref=src.at[peer],
                dst_ref=dst.at[k - 1],
                send_sem=send.at[k - 1],
                recv_sem=recv.at[k - 1],
                device_id={"hist": peer},
                device_id_type=pl.DeviceIdType.MESH,
            )
            copy.start()
            copies.append(copy)
    for copy in copies:
        copy.wait()
    logs = [stats[me]] + [got_stats[k] for k in range(n - 1)]
    highest = functools.reduce(jnp.maximum, logs)
    shares = [jnp.exp2(log - highest) for log in logs]
    inverse = 1.0 / functools.reduce(jnp.add, shares)
    embed = parts.shape[1]
    head = embed // H
    pieces = []
    for h in range(H):
        rows = slice(h * head, (h + 1) * head)
        mixed = parts[me, rows, :].astype(jnp.float32) * shares[0][h : h + 1, :]
        for k in range(n - 1):
            mixed += got[k, rows, :].astype(jnp.float32) * shares[k + 1][h : h + 1, :]
        pieces.append(mixed * inverse[h : h + 1, :])
    attended = jnp.concatenate(pieces, axis=0).astype(jnp.bfloat16)
    result[...] = lax.dot_general(
        attended, out_weight[3], (((0,), (0,)), ((), ())), preferred_element_type=jnp.float32
    ).astype(jnp.bfloat16)


def body(candidates, history, projections, lengths, selected):
    n = lax.axis_size("hist")
    ranks = lax.axis_size("dp")
    candidates, history, projections, lengths, selected = (
        pltpu.with_memory_space_constraint(x, pltpu.HBM) for x in (candidates, history, projections, lengths, selected)
    )
    users, own_cands, embed = candidates.shape
    cands = n * own_cands
    line = n // 2
    own_rows = history.shape[1]
    blocks = own_rows // BLOCK
    first = (lax.axis_index("hist") * blocks).astype(jnp.int32)
    base = first.reshape(1)
    weights, high, low, keys, values, flags = pl.pallas_call(
        functools.partial(gather_kernel, n, ranks),
        out_shape=[
            pltpu.VMEM((projections.shape[0], ranks * projections.shape[1], embed), jnp.bfloat16),
            pltpu.VMEM((users, embed, cands), jnp.bfloat16),
            pltpu.VMEM((users, embed, cands), jnp.bfloat16),
            pltpu.VMEM((users, own_rows, embed), jnp.bfloat16),
            pltpu.VMEM((users, embed, own_rows), jnp.bfloat16),
            jax.ShapeDtypeStruct((users, 128), jnp.int32),
        ],
        in_specs=[pl.BlockSpec(memory_space=pltpu.SMEM)] + [pl.BlockSpec(memory_space=pltpu.HBM)] * 4,
        out_specs=[pl.BlockSpec(memory_space=pltpu.VMEM)] * 6,
        scratch_shapes=[
            pltpu.VMEM(candidates.shape, jnp.bfloat16),
            pltpu.VMEM(projections.shape, jnp.bfloat16),
            pltpu.VMEM(selected.shape, jnp.int32),
            pltpu.VMEM((users, cands, embed), jnp.bfloat16),
            pltpu.VMEM((users, own_rows, embed), jnp.bfloat16),
            pltpu.SemaphoreType.DMA((users + 1,)),
            pltpu.SemaphoreType.DMA((3,)),
            pltpu.SemaphoreType.DMA((users,)),
            pltpu.SemaphoreType.DMA((line - 1, users)),
            pltpu.SemaphoreType.DMA((line - 1, users)),
            pltpu.SemaphoreType.DMA((line, users)),
            pltpu.SemaphoreType.DMA((line, users)),
            pltpu.SemaphoreType.DMA((ranks - 1,)),
            pltpu.SemaphoreType.DMA((ranks - 1,)),
        ],
        compiler_params=pltpu.CompilerParams(collective_id=1, has_side_effects=True, vmem_limit_bytes=ROOM),
        name="gather",
    )(lengths, candidates, projections, history, selected)
    wide = -(-users * own_cands // 128) * 128
    parts, stats = pl.pallas_call(
        functools.partial(attend_kernel, own_cands),
        in_specs=[pl.BlockSpec(memory_space=pltpu.SMEM)] * 3 + [pl.BlockSpec(memory_space=pltpu.VMEM)] * 4,
        out_specs=[pl.BlockSpec(memory_space=pltpu.VMEM)] * 2,
        scratch_shapes=[
            [pltpu.VMEM((users, 16, cands), jnp.bfloat16)] * H,
            [pltpu.VMEM((users, embed // H + 16, cands), jnp.float32)] * H,
            [pltpu.VMEM((users, 1, cands), jnp.float32)] * H,
            [pltpu.VMEM((users, 1, cands), jnp.float32)] * H,
            [pltpu.VMEM((PAIR * BLOCK, cands), jnp.bfloat16)] * 4,
            pltpu.SMEM(((users * blocks) + users * PAIR + 8 * PAIR,), jnp.int32),
            pltpu.SMEM((users * (blocks // PAIR + 1) + 8,), jnp.int32),
        ],
        out_shape=[
            pltpu.VMEM((n, embed, wide), jnp.bfloat16),
            pltpu.VMEM((n, H, wide), jnp.float32),
        ],
        compiler_params=pltpu.CompilerParams(vmem_limit_bytes=ROOM),
        name="attend",
    )(lengths, flags, base, high, low, keys, values)
    result = pl.pallas_call(
        functools.partial(combine_kernel, n),
        out_shape=jax.ShapeDtypeStruct((wide, embed), jnp.bfloat16),
        in_specs=[pl.BlockSpec(memory_space=pltpu.VMEM)] * 3,
        out_specs=pl.BlockSpec(memory_space=pltpu.VMEM),
        scratch_shapes=[
            pltpu.VMEM((n - 1, embed, wide), jnp.bfloat16),
            pltpu.VMEM((n - 1, H, wide), jnp.float32),
        ]
        + [pltpu.SemaphoreType.DMA((n - 1,))] * 4,
        compiler_params=pltpu.CompilerParams(collective_id=0, has_side_effects=True, vmem_limit_bytes=ROOM),
        name="combine",
    )(parts, stats, weights)
    return result[: users * own_cands].reshape(users, own_cands, embed)


def solution(mesh):
    placed = (
        P("dp", "hist", None),
        P("dp", "hist", None),
        P(None, "dp", None),
        P("dp"),
        P("dp", None),
    )
    return jax.shard_map(
        body, mesh=mesh, in_specs=placed, out_specs=P("dp", "hist", None), check_vma=False
    )
```

profile of v0, /device:TPU:10, one launch (start us, length us, event | category | flops | bytes accessed | tf_op | source)
XLA Modules:
  0.0 70.5 jit_solution(6135943031286236625)
XLA Ops:
  0.0 14.5 %gather.1 = (bf16[4,128,128]{2,1,0:T(8,128)(2,1)S(1)}, bf16[4,128,512]{2,1,0:T(8,128)(2,1)S(1)}, bf16[4,128,512]{2,1,0:T(8,128)(2,1)S(1)}, bf16[4,2048,128]{2,1,...) custom-call(s32[4]{0:T(128)} %lengths.3, bf16[4,64,128]{2,1,0:T(8,128)(2,1)} %cand_in.1, ...), custom_call_target="tpu_custom_call" | custom-call | tf_op jit(solution)/shard_map/gather/pallas_call | solution.py:393
  14.6 29.0 %attend.1 = (bf16[8,128,256]{2,1,0:T(8,128)(2,1)S(1)}, f32[8,4,256]{2,1,0:T(4,128)S(1)}) custom-call(s32[4]{0:T(128)} %lengths.3, s32[4,128]{1,0:T(4,128)S(1)} %get-tuple-element.13.flags, s32[1]{0:T(128)} %bitcast.base, bf16[4,128,512]{2,1,0:T(8,128)(2,1)S(1)} %get-tuple-element.14.high, bf16[4,128,512]{2,1,0:T(8,128)(2,1)S(1)} %get-tuple-element.15.low, ...), custom_call_target="tpu_custom_call" | custom-call | tf_op jit(solution)/shard_map/attend/pallas_call | solution.py:425
  43.6 26.3 %combine.1 = bf16[256,128]{1,0:T(8,128)(2,1)S(1)} custom-call(bf16[8,128,256]{2,1,0:T(8,128)(2,1)S(1)} %get-tuple-element.18.parts, f32[8,4,256]{2,1,0:T(4,128)S(1)} %get-tuple-element.19.stats, bf16[4,128,128]{2,1,0:T(8,128)(2,1)S(1)} %get-tuple-element.20.out_weight), custom_call_target="tpu_custom_call" | custom-call | tf_op jit(solution)/shard_map/combine/pallas_call | solution.py:445
  69.9 0.6 copy.7
where the time goes:
time: 71 us; the launch traced here: 70.5 us
  Pallas kernels  69.8 us (98%)
    pallas_call x1, Pallas kernels, body(): pl.pallas_call(functools.partial(attend_kernel, own_cands), in_specs=[pl....  29 us
    pallas_call x1, Pallas kernels, body(): pl.pallas_call(functools.partial(combine_kernel, n), out_shape=jax.ShapeD...  26.3 us
    pallas_call x1, Pallas kernels, body(): pl.pallas_call(functools.partial(gather_kernel, n, ranks), out_shape=[plt...  14.5 us

commit v1 on v0

--- a/solution.py
+++ b/solution.py
@@ -30,8 +30,7 @@
     hist,
     picks_in,
     all_proj,
-    high,
-    low,
+    query,
     keys,
     values,
     flags,
@@ -58,7 +57,6 @@
     rows = proj.shape[1]
     own_rows, embed = hist.shape[1], hist.shape[2]
     blocks = own_rows // BLOCK
-    factor = math.log2(math.e) / math.sqrt(embed // H)
 
     def place(u, owner):
         return all_cand.at[u, pl.ds(pl.multiple_of(owner * own, own), own), :]
@@ -162,13 +160,9 @@
         for k in range(line):
             across[k, u].wait_recv()
         locals_[1 + u].wait()
-        plain = lax.dot_general(
+        query[u] = lax.dot_general(
             all_proj[0], all_cand[u], (((0,), (1,)), ((), ())), preferred_element_type=jnp.float32
         ).astype(jnp.bfloat16)
-        scaled = plain.astype(jnp.float32) * factor
-        upper = scaled.astype(jnp.bfloat16)
-        high[u] = upper
-        low[u] = (scaled - upper.astype(jnp.float32)).astype(jnp.bfloat16)
     for copy in list(along.values()) + list(across.values()):
         copy.wait_send()
 
@@ -178,13 +172,11 @@
     lengths,
     flags,
     base,
-    high,
-    low,
+    query,
     keys,
     values,
     parts,
     stats,
-    marks,
     acc,
     shift,
     top,
@@ -192,11 +184,11 @@
     slots,
     owners,
 ):
-    users, embed, cands = high.shape
+    users, embed, cands = query.shape
     head = embed // H
-    half = embed // 2
     tall = acc[0].shape[1]
     blocks = keys.shape[1] // BLOCK
+    factor = math.log2(math.e) / math.sqrt(head)
     first = base[0]
 
     owners[0] = 0
@@ -226,22 +218,16 @@
         return pl.multiple_of(block * BLOCK, BLOCK)
 
     column = lax.broadcasted_iota(jnp.int32, (1, embed), 1)
-    group = [(h * head) // half for h in range(H)]
-    spot = [(1 - group[h]) * half + (h - group[h] * (H // 2)) * 16 for h in range(H)]
     mine = [jnp.where(column // head == h, 1.0, 0.0).astype(jnp.bfloat16) for h in range(H)]
-    mark = [jnp.where(column == spot[h], 1.0, 0.0).astype(jnp.bfloat16) for h in range(H)]
-    lead = lax.broadcasted_iota(jnp.int32, (16, cands), 0) == 0
 
     for u in range(users):
         sample = keys[u, pl.ds(start_of(slots[begins[u] * PAIR]), SAMPLE), :]
         guess = jnp.dot(
-            jnp.concatenate([sample * mine[h] for h in range(H)], axis=0), high[u], preferred_element_type=jnp.float32
+            jnp.concatenate([sample * mine[h] for h in range(H)], axis=0), query[u], preferred_element_type=jnp.float32
         )
         for h in range(H):
             most = jnp.max(guess[h * SAMPLE : (h + 1) * SAMPLE, :], axis=0, keepdims=True)
-            most = most.astype(jnp.bfloat16).astype(jnp.float32)
-            shift[h][u] = most
-            marks[h][u] = jnp.where(lead, -most, 0.0).astype(jnp.bfloat16)
+            shift[h][u] = most * factor
     for h in range(H):
         acc[h][...] = jnp.zeros(acc[h].shape, jnp.float32)
     for k in range(2):
@@ -254,13 +240,8 @@
     def scores(i, h):
         user = owners[i]
         key = jnp.concatenate([keys[user, pl.ds(start_of(slots[i * PAIR + k]), BLOCK), :] for k in range(PAIR)], axis=0)
-        key = key * mine[h]
-        pieces = [high[user]]
-        if spot[h] > 0:
-            pieces.append(low[user, 0 : spot[h], :])
-        pieces += [marks[h][user], low[user, spot[h] + 16 : embed, :]]
-        query = jnp.concatenate(pieces, axis=0)
-        return jnp.dot(jnp.concatenate([key, key + mark[h]], axis=1), query, preferred_element_type=jnp.float32)
+        got = jnp.dot(key * mine[h], query[user], preferred_element_type=jnp.float32)
+        return got * factor - shift[h][user]
 
     def gain(i, h, prob):
         user = owners[i]
@@ -390,18 +371,17 @@
     blocks = own_rows // BLOCK
     first = (lax.axis_index("hist") * blocks).astype(jnp.int32)
     base = first.reshape(1)
-    weights, high, low, keys, values, flags = pl.pallas_call(
+    weights, query, keys, values, flags = pl.pallas_call(
         functools.partial(gather_kernel, n, ranks),
         out_shape=[
             pltpu.VMEM((projections.shape[0], ranks * projections.shape[1], embed), jnp.bfloat16),
-            pltpu.VMEM((users, embed, cands), jnp.bfloat16),
             pltpu.VMEM((users, embed, cands), jnp.bfloat16),
             pltpu.VMEM((users, own_rows, embed), jnp.bfloat16),
             pltpu.VMEM((users, embed, own_rows), jnp.bfloat16),
             jax.ShapeDtypeStruct((users, 128), jnp.int32),
         ],
         in_specs=[pl.BlockSpec(memory_space=pltpu.SMEM)] + [pl.BlockSpec(memory_space=pltpu.HBM)] * 4,
-        out_specs=[pl.BlockSpec(memory_space=pltpu.VMEM)] * 6,
+        out_specs=[pl.BlockSpec(memory_space=pltpu.VMEM)] * 5,
         scratch_shapes=[
             pltpu.VMEM(candidates.shape, jnp.bfloat16),
             pltpu.VMEM(projections.shape, jnp.bfloat16),
@@ -424,10 +404,9 @@
     wide = -(-users * own_cands // 128) * 128
     parts, stats = pl.pallas_call(
         functools.partial(attend_kernel, own_cands),
-        in_specs=[pl.BlockSpec(memory_space=pltpu.SMEM)] * 3 + [pl.BlockSpec(memory_space=pltpu.VMEM)] * 4,
+        in_specs=[pl.BlockSpec(memory_space=pltpu.SMEM)] * 3 + [pl.BlockSpec(memory_space=pltpu.VMEM)] * 3,
         out_specs=[pl.BlockSpec(memory_space=pltpu.VMEM)] * 2,
         scratch_shapes=[
-            [pltpu.VMEM((users, 16, cands), jnp.bfloat16)] * H,
             [pltpu.VMEM((users, embed // H + 16, cands), jnp.float32)] * H,
             [pltpu.VMEM((users, 1, cands), jnp.float32)] * H,
             [pltpu.VMEM((users, 1, cands), jnp.float32)] * H,
@@ -441,7 +420,7 @@
         ],
         compiler_params=pltpu.CompilerParams(vmem_limit_bytes=ROOM),
         name="attend",
-    )(lengths, flags, base, high, low, keys, values)
+    )(lengths, flags, base, query, keys, values)
     result = pl.pallas_call(
         functools.partial(combine_kernel, n),
         out_shape=jax.ShapeDtypeStruct((wide, embed), jnp.bfloat16),

time: 71 us -> 65.5 us (0.923)
  the two profiles are of different devices: /device:TPU:10 before, /device:TPU:8 now
where the time goes in v1:
time: 65.5 us; the launch traced here: 65.2 us
  Pallas kernels  64.5 us (98%)
    pallas_call x1, Pallas kernels, body(): pl.pallas_call(functools.partial(attend_kernel, own_cands), in_specs=[pl....  34.1 us
    pallas_call x1, Pallas kernels, body(): pl.pallas_call(functools.partial(combine_kernel, n), out_shape=jax.ShapeD...  15.4 us
    pallas_call x1, Pallas kernels, body(): pl.pallas_call(functools.partial(gather_kernel, n, ranks), out_shape=[plt...  15 us

profile of v1, /device:TPU:8, one launch (start us, length us, event | category | flops | bytes accessed | tf_op | source)
XLA Modules:
  0.0 65.2 jit_solution(11874603497791726366)
XLA Ops:
  0.0 15.0 %gather.1 = (bf16[4,128,128]{2,1,0:T(8,128)(2,1)S(1)}, bf16[4,128,512]{2,1,0:T(8,128)(2,1)S(1)}, bf16[4,2048,128]{2,1,0:T(8,128)(2,1)S(1)}, bf16[4,128,2048]{2,1,0:T(8,128)(2,1)S(1)}, s32[4,128]{1,0:T(4,128)S(1)}) custom-call(s32[4]{0:T(128)} %lengths.3, bf16[4,64,128]{2,1,0:T(8,128)(2,1)} %cand_in.1, bf16[4,32,128]{2,1,0:T(8,128)(2,1)} %proj_in.1, ...), custom_call_target="tpu_custom_call" | custom-call | tf_op jit(solution)/shard_map/gather/pallas_call | solution.py:374
  15.0 34.1 %attend.1 = (bf16[8,128,256]{2,1,0:T(8,128)(2,1)S(1)}, f32[8,4,256]{2,1,0:T(4,128)S(1)}) custom-call(s32[4]{0:T(128)} %lengths.3, s32[4,128]{1,0:T(4,128)S(1)} %get-tuple-element.12.flags, s32[1]{0:T(128)} %bitcast.base, bf16[4,128,512]{2,1,0:T(8,128)(2,1)S(1)} %get-tuple-element.13.query, bf16[4,2048,128]{2,1,0:T(8,128)(2,1)S(1)} %get-tuple-element.14.keys, ...), custom_call_target="tpu_custom_call" | custom-call | tf_op jit(solution)/shard_map/attend/pallas_call | solution.py:405
  49.2 15.4 %combine.1 = bf16[256,128]{1,0:T(8,128)(2,1)S(1)} custom-call(bf16[8,128,256]{2,1,0:T(8,128)(2,1)S(1)} %get-tuple-element.16.parts, f32[8,4,256]{2,1,0:T(4,128)S(1)} %get-tuple-element.17.stats, bf16[4,128,128]{2,1,0:T(8,128)(2,1)S(1)} %get-tuple-element.18.out_weight), custom_call_target="tpu_custom_call" | custom-call | tf_op jit(solution)/shard_map/combine/pallas_call | solution.py:424
  64.5 0.6 copy.7
